TPU v7x, 16 devices: a 4x2x1 block of a 4x4x8 slice. The times are simulated.
16 devices in a mesh: rep: 4 (over y, z, core), dp: 4 (over x).
Axes of the slice: x: 4, y: 2, z: 1, core: 2. Of those that a mesh axis runs over, the one named last changes fastest.
The devices are a block of a 4x4x8 slice.
Arguments:
- a: bfloat16 [16, 4, 8192, 512], P(('rep', 'dp')), parts along dimension 0
- g: bfloat16 [16, 4, 8192, 1280], P(('rep', 'dp')), parts along dimension 0
Outputs:
- output: bfloat16 [16, 512, 1280], P('rep'), parts along dimension 0
There are 4 independent parts. A program takes and returns all parts, laid end to end along the dimension named above; each array names one.
All inputs are finite; a program needn't handle non-finite values.
Results may differ from a plain program's by a relative error of at most 0.012.
Values are sent between devices in bfloat16 or wider.
A program may use at most 768 MiB of HBM per device.

v0:
```python
import jax
import jax.numpy as jnp


def solution(mesh):
    groups = mesh.shape["rep"]

    def step(a, g):
        a, g = (t.reshape(groups, -1, *t.shape[1:]) for t in (a, g))
        sums = jnp.einsum("rsntd,rsntf->rndf", a, g, preferred_element_type=jnp.float32)
        return sums.astype(jnp.bfloat16).reshape(-1, *sums.shape[2:])

    return step
```

profile of v0, /device:TPU:112, one launch (start us, length us, event | category | flops | bytes accessed | tf_op | source)
XLA Modules:
  0.0 240.6 jit_solution(9263503347643265050)
XLA Ops:
  0.0 55.4 %fusion.3 = f32[1,4,512,1280]{3,2,1,0:T(8,128)} fusion(bf16[1,4,8192,1280]{3,2,1,0:T(8,128)(2,1)} %param.1, bf16[1,4,8192,512]{3,2,1,0:T(8,128)(2,1)} %param), kind=kOutput, calls=%fused_computation.3 | convolution fusion | flops 42949672960 | bytes 127926272 | tf_op jit(solution)/rsntd,rsntf->rndf/dot_general | solution.py:10
  55.4 185.2 %all-reduce.2 = bf16[1,4,512,1280]{3,2,1,0:T(8,128)(2,1)} all-reduce(f32[1,4,512,1280]{3,2,1,0:T(8,128)} %fusion.3), channel_id=1, replica_groups=[4,4]<=[16], use_global_device_ids=true, to_apply=%add.clone | all-reduce | flops 2621440 | bytes 15728640 | tf_op jit(solution)/rsntd,rsntf->rndf/dot_general | solution.py:10
where the time goes:
time: 241 us
  blocking collectives  185 us (77%)
  matrix products  55.4 us (23%)
    dot_general x1, blocking collectives, step(): jnp.einsum('rsntd,rsntf->rndf', a, g, preferred_element_type=jnp.float32)  185 us
    dot_general x1, matrix products, step(): jnp.einsum('rsntd,rsntf->rndf', a, g, preferred_element_type=jnp.float32)  55.4 us

commit v1 on v0

v1 whole, which is shorter than its diff:
```python
import functools

import jax
import jax.numpy as jnp
from jax import lax
from jax.experimental import pallas as pl
from jax.experimental.pallas import tpu as pltpu
from jax.sharding import PartitionSpec as P

C = 256
KF = 1
GS = 3
LF, LO = 2, 4
AG_EVERY = 2
MESH = pl.DeviceIdType.MESH
F32, BF16 = jnp.float32, jnp.bfloat16


def kernel(ring, a_hbm, g_hbm, o_ref, abuf, gbuf, acc, far_s, mid_s, leaf_s, far_r, mid_r, leaf_r,
           a_sem, g_sem, ss, rs):
    mats, tokens, d = a_hbm.shape
    cols = g_hbm.shape[2] // C
    units = mats * cols
    rows = d // ring
    kt = tokens // KF
    me = lax.axis_index("dp")

    def at(x):
        return lax.rem(me + x + 2 * ring, ring)

    def a_copy(n, k):
        t = pl.ds(k * kt, kt)
        return pltpu.make_async_copy(a_hbm.at[n, t], abuf.at[lax.rem(n, 2), t], a_sem.at[lax.rem(n, 2), k])

    def g_copy(u, k):
        n, j = lax.div(u, cols), lax.rem(u, cols)
        t = pl.ds(k * kt, kt)
        return pltpu.make_async_copy(
            g_hbm.at[n, t, pl.ds(pl.multiple_of(j * C, C), C)], gbuf.at[lax.rem(u, GS), t], g_sem.at[lax.rem(u, GS), k])

    def i32(x):
        return jnp.int32(x)

    for k in range(KF):
        a_copy(i32(0), k).start()
        g_copy(i32(0), k).start()
    for k in range(KF):
        g_copy(i32(1), k).start()

    barrier = pltpu.get_barrier_semaphore()
    for x in (1, -1):
        pl.semaphore_signal(barrier, inc=1, device_id={"dp": at(x)}, device_id_type=MESH)
    pl.semaphore_wait(barrier, 2)

    def sign(u):
        return 1 - 2 * lax.rem(u, 2)

    def block(u, r):
        return o_ref.at[lax.div(u, cols), pl.ds(pl.multiple_of(r * rows, rows), rows),
                        pl.ds(pl.multiple_of(lax.rem(u, cols) * C, C), C)]

    def far(u):
        return pltpu.make_async_remote_copy(far_s.at[u], far_r.at[u], ss.at[0, u], rs.at[0, u],
                                            device_id={"dp": at(sign(u))}, device_id_type=MESH)

    def leaf(u):
        return pltpu.make_async_remote_copy(leaf_s.at[u], leaf_r.at[u], ss.at[1, u], rs.at[1, u],
                                            device_id={"dp": at(-sign(u))}, device_id_type=MESH)

    def mid(u):
        return pltpu.make_async_remote_copy(mid_s.at[u], mid_r.at[u], ss.at[2, u], rs.at[2, u],
                                            device_id={"dp": at(sign(u))}, device_id_type=MESH)

    def gather(u, i, owner, x):
        b = block(u, owner)
        return pltpu.make_async_remote_copy(b, b, ss.at[3 + i, u], rs.at[3 + i, u],
                                            device_id={"dp": at(x)}, device_id_type=MESH)

    def term(u, r):
        return acc[lax.rem(u, LO + 1), pl.ds(pl.multiple_of(r * rows, rows), rows)]

    def do_raw(u):
        s = sign(u)
        far_s[u] = term(u, at(2)).astype(BF16)
        far(u).start()
        leaf_s[u] = term(u, at(-s)).astype(BF16)
        leaf(u).start()

    def do_mid(u):
        far(u).wait_recv()
        mid_s[u] = (term(u, at(sign(u))) + far_r[u].astype(F32)).astype(BF16)
        mid(u).start()

    def do_own(u):
        leaf(u).wait_recv()
        mid(u).wait_recv()
        block(u, me)[...] = (term(u, me) + mid_r[u].astype(F32) + leaf_r[u].astype(F32)).astype(BF16)

    def do_gather(u):
        s = sign(u)
        gather(u, 0, me, -s).start()
        gather(u, 1, me, s).start()

    def do_pass(u):
        s = sign(u)
        gather(u, 0, at(s), -s).wait_recv()
        gather(u, 2, at(s), -s).start()

    def done(u):
        s = sign(u)
        gather(u, 1, at(-s), s).wait_recv()
        gather(u, 2, at(2), -s).wait_recv()
        far(u).wait_send()
        leaf(u).wait_send()
        mid(u).wait_send()
        for i in range(3):
            gather(u, i, me, s).wait_send()

    wait = -(-LO // AG_EVERY)
    dims = (((0,), (0,)), ((), ()))

    def slot(u, carry):
        n, j = lax.div(u, cols), lax.rem(u, cols)

        @pl.when(u + 2 < units)
        def _():
            for k in range(KF):
                g_copy(u + 2, k).start()

        @pl.when((j < KF) & (n + 1 < mats))
        def _():
            a_copy(n + 1, j).start()

        sl, gl, cl = lax.rem(n, 2), lax.rem(u, GS), lax.rem(u, LO + 1)
        for k in range(KF):
            g_copy(u, k).wait()

            @pl.when(j == 0)
            def _():
                a_copy(n, k).wait()
            t = pl.ds(k * kt, kt)
            p = lax.dot_general(abuf[sl, t], gbuf[gl, t], dims, preferred_element_type=F32)
            if k:
                acc[cl] += p
            else:
                acc[cl] = p
        do_raw(u)

        @pl.when(u >= LF)
        def _():
            do_mid(u - LF)

        @pl.when(u >= LO)
        def _():
            do_own(u - LO)

        @pl.when((lax.rem(u, AG_EVERY) == 0) & (u >= wait * AG_EVERY))
        def _():
            do_gather(lax.div(u, AG_EVERY) - wait)
        return carry

    lax.fori_loop(0, units, slot, 0)
    sent = (units - 1) // AG_EVERY - wait + 1
    c = lambda f: (lambda u, _: (f(u), _)[1])
    lax.fori_loop(units - LF, units, c(do_mid), 0)
    lax.fori_loop(sent, sent + 4, c(do_gather), 0)
    lax.fori_loop(units - LO, units, c(do_own), 0)
    lax.fori_loop(sent + 4, units, c(do_gather), 0)
    lax.fori_loop(0, units, c(do_pass), 0)
    lax.fori_loop(0, units, c(done), 0)


def solution(mesh):
    ring = mesh.shape["dp"]

    def body(a, g):
        _, mats, tokens, d = a.shape
        ff = g.shape[-1]
        units, rows = mats * (ff // C), d // ring
        blk = pltpu.VMEM((units, rows, C), BF16)
        return pl.pallas_call(
            functools.partial(kernel, ring),
            out_shape=pltpu.VMEM((mats, d, ff), BF16),
            in_specs=[pl.BlockSpec(memory_space=pl.ANY)] * 2,
            out_specs=pl.BlockSpec(memory_space=pltpu.VMEM),
            scratch_shapes=[
                pltpu.VMEM((2, tokens, d), BF16),
                pltpu.VMEM((GS, tokens, C), BF16),
                pltpu.VMEM((LO + 1, d, C), F32),
                blk, blk, blk, blk, blk, blk,
                pltpu.SemaphoreType.DMA((2, KF)),
                pltpu.SemaphoreType.DMA((GS, KF)),
                pltpu.SemaphoreType.DMA((6, units)),
                pltpu.SemaphoreType.DMA((6, units)),
            ],
            compiler_params=pltpu.CompilerParams(
                collective_id=0, has_side_effects=True, vmem_limit_bytes=46 << 20),
            cost_estimate=pl.CostEstimate(
                flops=2 * mats * tokens * d * ff, bytes_accessed=2 * mats * tokens * (d + ff), transcendentals=0),
        )(a[0], g[0])

    return jax.shard_map(body, mesh=mesh, in_specs=P(("rep", "dp")), out_specs=P("rep"), check_vma=False)
```

time: 241 us -> 104 us (0.43)
  blocking collectives: 185 us -> 0 us
  Pallas kernels: 0 us -> 101 us
  matrix products: 55.4 us -> 0 us
    dot_general x1 -> x0, blocking collectives: 185 us -> none  [step(): jnp.einsum('rsntd,rsntf->rndf', a, g, preferred_element_type=jnp.float32)]
    pallas_call x0 -> x1, Pallas kernels: none -> 101 us  [body(): pl.pallas_call(functools.partial(kernel, ring), out_shape=pltpu.VMEM((mat...]
    dot_general x1 -> x0, matrix products: 55.4 us -> none  [step(): jnp.einsum('rsntd,rsntf->rndf', a, g, preferred_element_type=jnp.float32)]
where the time goes in v1:
time: 104 us; the launch traced here: 103 us
  Pallas kernels  101 us (97%)
  local copies, waits for them, and re-layouts  2.36 us (2%)
    pallas_call x1, Pallas kernels, body(): pl.pallas_call(functools.partial(kernel, ring), out_shape=pltpu.VMEM((mat...  101 us
    unnamed x1, local copies, waits for them, and re-layouts  2.36 us

profile of v1, /device:TPU:112, one launch (start us, length us, event | category | flops | bytes accessed | tf_op | source)
XLA Modules:
  0.0 103.5 jit_solution(2002073093897799562)
XLA Ops:
  0.0 101.1 %shard_map.28 = bf16[4,512,1280]{2,1,0:T(8,128)(2,1)S(1)} custom-call(bf16[4,8192,512]{2,1,0:T(8,128)(2,1)} %bitcast.2, bf16[4,8192,1280]{2,1,0:T(8,128)(2,1)} %bitcast.1.g_hbm), custom_call_target="tpu_custom_call" | custom-call | flops 42949672960 | bytes 117440512 | tf_op jit(solution)/shard_map/pallas_call | solution.py:181
  101.1 2.4 %copy.4 = bf16[4,512,1280]{2,1,0:T(8,128)(2,1)} copy(bf16[4,512,1280]{2,1,0:T(8,128)(2,1)S(1)} %shard_map.28) | data formatting | bytes 10485760

commit v2 on v0

v2 whole, which is shorter than its diff:
```python
import functools

import jax
import jax.numpy as jnp
from jax import lax
from jax.experimental import pallas as pl
from jax.experimental.pallas import tpu as pltpu
from jax.sharding import PartitionSpec as P

C = 256
LEAD = 2
AHEAD = 2
GS = LEAD + AHEAD + 1
LO = 2
AG_EVERY = 2
AG_HEAD = 4
KS = 1
MESH = pl.DeviceIdType.MESH
F32, BF16 = jnp.float32, jnp.bfloat16
DIMS = (((0,), (0,)), ((), ()))


def kernel(ring, a_hbm, g_hbm, o_ref, abuf, gbuf, own, far_s, mid_s, leaf_s, far_r, mid_r, leaf_r,
           part, a_sem, g_sem, k_sem, ss, rs):
    mats, tokens, d = a_hbm.shape
    cols = g_hbm.shape[2] // C
    units = mats * cols
    rows = d // ring
    me = lax.axis_index("dp")

    def at(x):
        return lax.rem(me + x + ring, ring)

    def col(r, width):
        return pl.ds(pl.multiple_of(r * width, width), width)

    def a_copy(n, x):
        sl = lax.rem(n, 2)
        return pltpu.make_async_copy(a_hbm.at[n, :, col(at(x), rows)], abuf.at[sl, x], a_sem.at[sl, x])

    def g_copy(u):
        sl = lax.rem(u, GS)
        return pltpu.make_async_copy(g_hbm.at[lax.div(u, cols), :, col(lax.rem(u, cols), C)], gbuf.at[sl], g_sem.at[sl])

    def i32(x):
        return jnp.int32(x)

    def piece(i, k):
        t = pl.ds(k * (tokens // KS), tokens // KS)
        if i == 2:
            return pltpu.make_async_copy(g_hbm.at[0, t, pl.ds(0, C)], gbuf.at[0, t], k_sem.at[2, k])
        x = 2 + i
        return pltpu.make_async_copy(a_hbm.at[0, t, col(at(x), rows)], abuf.at[0, x, t], k_sem.at[i, k])

    for k in range(KS):
        for i in range(3):
            piece(i, k).start()
    a_copy(i32(0), 1).start()
    for u in range(1, AHEAD + 1):
        g_copy(i32(u)).start()
    a_copy(i32(0), 0).start()

    barrier = pltpu.get_barrier_semaphore()
    for x in (1, -1):
        pl.semaphore_signal(barrier, inc=1, device_id={"dp": at(x)}, device_id_type=MESH)

    def remote(src, dst, i, u, x):
        return pltpu.make_async_remote_copy(src, dst, ss.at[i, u], rs.at[i, u], device_id={"dp": at(x)}, device_id_type=MESH)

    def block(u, r):
        return o_ref.at[lax.div(u, cols), col(r, rows), col(lax.rem(u, cols), C)]

    def far(u, s):
        return remote(far_s.at[u], far_r.at[u], 0, u, s)

    def leaf(u, s):
        return remote(leaf_s.at[u], leaf_r.at[u], 1, u, -s)

    def mid(u, s):
        return remote(mid_s.at[u], mid_r.at[u], 2, u, s)

    def gather(u, i, owner, x):
        return remote(block(u, owner), block(u, owner), 3 + i, u, x)

    def sign(u):
        return 1 - 2 * lax.rem(u, 2)

    def beside(s):
        return lax.rem(ring - s, ring)

    def terms(u, x, y):
        sl = lax.rem(lax.div(u, cols), 2)
        lhs = jnp.concatenate([abuf[sl, x], abuf[sl, y]], axis=1)
        return lax.dot_general(lhs, gbuf[lax.rem(u, GS)], DIMS, preferred_element_type=F32)

    def send(u, s, p):
        far_s[u] = p[:rows].astype(BF16)
        far(u, s).start()
        leaf_s[u] = p[rows:].astype(BF16)
        leaf(u, s).start()

    def first(u):
        n, j, s = lax.div(u, cols), lax.rem(u, cols), sign(u)

        @pl.when(u + AHEAD < units)
        def _():
            g_copy(u + AHEAD).start()

        @pl.when((j == LEAD) & (n + 1 < mats))
        def _():
            a_copy(n + 1, 2).start()
            a_copy(n + 1, 3).start()

        @pl.when((j == LEAD + 1) & (n + 1 < mats))
        def _():
            a_copy(n + 1, 1).start()
            a_copy(n + 1, 0).start()

        @pl.when((j == 0) & (n > 0))
        def _():
            a_copy(n, 2).wait()
            a_copy(n, 3).wait()
            a_copy(n, 1).wait()

        @pl.when(u == 1)
        def _():
            a_copy(n, 1).wait()

        g_copy(u).wait()
        send(u, s, terms(u, 2, beside(s)))

    def second(u):
        s = sign(u)

        @pl.when(lax.rem(u, cols) == 0)
        def _():
            a_copy(lax.div(u, cols), 0).wait()

        p = terms(u, beside(-s), 0)
        own[lax.rem(u, LO + 1)] = p[rows:]
        far(u, s).wait_recv()
        mid_s[u] = (p[:rows] + far_r[u].astype(F32)).astype(BF16)
        mid(u, s).start()

    def finish(u):
        leaf(u, sign(u)).wait_recv()
        mid(u, sign(u)).wait_recv()
        block(u, me)[...] = (own[lax.rem(u, LO + 1)] + mid_r[u].astype(F32) + leaf_r[u].astype(F32)).astype(BF16)

    def spread(u):
        gather(u, 0, me, -sign(u)).start()
        gather(u, 1, me, sign(u)).start()

    def hand_on(u):
        s = sign(u)
        gather(u, 0, at(s), -s).wait_recv()
        gather(u, 2, at(s), -s).start()

    def done(u):
        s = sign(u)
        gather(u, 1, at(-s), s).wait_recv()
        gather(u, 2, at(2), -s).wait_recv()
        far(u, s).wait_send()
        leaf(u, s).wait_send()
        mid(u, s).wait_send()
        for i in range(3):
            gather(u, i, me, s).wait_send()

    wait = -(-LO // AG_EVERY)

    for k in range(KS):
        for i in range(3):
            piece(i, k).wait()
        t = pl.ds(k * (tokens // KS), tokens // KS)
        lhs = jnp.concatenate([abuf[0, 2, t], abuf[0, 3, t]], axis=1)
        p = lax.dot_general(lhs, gbuf[0, t], DIMS, preferred_element_type=F32)
        if k == 0:
            part[...] = p
        elif k < KS - 1:
            part[...] += p
    pl.semaphore_wait(barrier, 2)
    send(i32(0), 1, p)

    def step(u, carry):
        v = u - LEAD

        @pl.when(u < units)
        def _():
            first(u)

        @pl.when(v >= 0)
        def _():
            second(v)

        @pl.when(v >= LO)
        def _():
            finish(v - LO)

        @pl.when((lax.rem(v, AG_EVERY) == 0) & (v >= wait * AG_EVERY))
        def _():
            spread(lax.div(v, AG_EVERY) - wait)
        return carry

    lax.fori_loop(1, units + LEAD, step, 0)
    sent = (units - 1) // AG_EVERY - wait + 1

    def each(f, lo, hi):
        def body(u, carry):
            f(u)
            return carry
        lax.fori_loop(lo, hi, body, 0)

    each(spread, sent, sent + AG_HEAD)
    each(finish, units - LO, units)
    each(spread, sent + AG_HEAD, units)
    each(hand_on, 0, units)
    each(done, 0, units)


def solution(mesh):
    ring = mesh.shape["dp"]

    def body(a, g):
        _, mats, tokens, d = a.shape
        ff = g.shape[-1]
        units, rows = mats * (ff // C), d // ring
        blk = pltpu.VMEM((units, rows, C), BF16)
        return pl.pallas_call(
            functools.partial(kernel, ring),
            out_shape=pltpu.VMEM((mats, d, ff), BF16),
            in_specs=[pl.BlockSpec(memory_space=pl.ANY)] * 2,
            out_specs=pl.BlockSpec(memory_space=pltpu.VMEM),
            scratch_shapes=[
                pltpu.VMEM((2, ring, tokens, rows), BF16),
                pltpu.VMEM((GS, tokens, C), BF16),
                pltpu.VMEM((LO + 1, rows, C), F32),
                blk, blk, blk, blk, blk, blk,
                pltpu.VMEM((2 * rows, C), F32),
                pltpu.SemaphoreType.DMA((2, ring)),
                pltpu.SemaphoreType.DMA((GS,)),
                pltpu.SemaphoreType.DMA((3, KS)),
                pltpu.SemaphoreType.DMA((6, units)),
                pltpu.SemaphoreType.DMA((6, units)),
            ],
            compiler_params=pltpu.CompilerParams(
                collective_id=0, has_side_effects=True, vmem_limit_bytes=50 << 20),
            cost_estimate=pl.CostEstimate(
                flops=2 * mats * tokens * d * ff, bytes_accessed=2 * mats * tokens * (d + ff), transcendentals=0),
        )(a[0], g[0])

    return jax.shard_map(body, mesh=mesh, in_specs=P(("rep", "dp")), out_specs=P("rep"), check_vma=False)
```

time: 241 us -> 100 us (0.41)
  blocking collectives: 185 us -> 0 us
  Pallas kernels: 0 us -> 97.7 us
  matrix products: 55.4 us -> 0 us
    dot_general x1 -> x0, blocking collectives: 185 us -> none  [step(): jnp.einsum('rsntd,rsntf->rndf', a, g, preferred_element_type=jnp.float32)]
    pallas_call x0 -> x1, Pallas kernels: none -> 97.7 us  [body(): pl.pallas_call(functools.partial(kernel, ring), out_shape=pltpu.VMEM((mat...]
    dot_general x1 -> x0, matrix products: 55.4 us -> none  [step(): jnp.einsum('rsntd,rsntf->rndf', a, g, preferred_element_type=jnp.float32)]
where the time goes in v2:
time: 100 us
  Pallas kernels  97.7 us (98%)
  local copies, waits for them, and re-layouts  2.36 us (2%)
    pallas_call x1, Pallas kernels, body(): pl.pallas_call(functools.partial(kernel, ring), out_shape=pltpu.VMEM((mat...  97.7 us
    unnamed x1, local copies, waits for them, and re-layouts  2.36 us

profile of v2, /device:TPU:112, one launch (start us, length us, event | category | flops | bytes accessed | tf_op | source)
XLA Modules:
  0.0 100.1 jit_solution(15312343232227070906)
XLA Ops:
  0.0 97.7 %shard_map.28 = bf16[4,512,1280]{2,1,0:T(8,128)(2,1)S(1)} custom-call(bf16[4,8192,512]{2,1,0:T(8,128)(2,1)} %bitcast.2, bf16[4,8192,1280]{2,1,0:T(8,128)(2,1)} %bitcast.1.g_hbm), custom_call_target="tpu_custom_call" | custom-call | flops 42949672960 | bytes 117440512 | tf_op jit(solution)/shard_map/pallas_call | solution.py:228
  97.7 2.4 %copy.4 = bf16[4,512,1280]{2,1,0:T(8,128)(2,1)} copy(bf16[4,512,1280]{2,1,0:T(8,128)(2,1)S(1)} %shard_map.28) | data formatting | bytes 10485760
